TPU v7x, 128 devices: a whole 4x4x4 slice. The times are simulated.
128 devices in a mesh: rep: 2 (over z_hi), shard: 64 (over y, z_lo, x, core).
Axes of the slice: x: 4, y: 4, z: 4 (z_hi: 2, z_lo: 2; z = z_hi * 2 + z_lo), core: 2. Of those that a mesh axis runs over, the one named last changes fastest.
Arguments:
- dense: bfloat16 [32768, 128], P(('rep', 'shard')), may hold values from -6 to 6
- small_ids: int32 [32768, 32], P(('rep', 'shard')), may hold values from 0 to 511
- labels: int32 [32768], P(('rep', 'shard')), may hold values 0 or 1
- small_tables: bfloat16 [32, 512, 128], replicated, may hold values from -6 to 6
- large_tables: bfloat16 [64, 8192, 128], P('shard'), may hold values from -6 to 6
- batch_sizes: int32 [64, 128], replicated, may hold values from 1 to 128, as said below
- bag_ends: int32 [64, 128, 128], P('shard'), may hold values from 0 to 256, as said below
- owner_row_index: int32 [64, 128, 256], P('shard'), may hold values from 0 to 8191
- w_first: bfloat16 [4784, 1024], replicated, may hold values from -0.09375 to 0.09375
- b_first: float32 [1024], replicated, may hold values from -3 to 3
- w_out: float32 [1024], replicated, may hold values from -0.1875 to 0.1875
Outputs:
- small_new: bfloat16 [32, 512, 128], replicated
- large_new: bfloat16 [64, 8192, 128], P('shard')
Inputs may be any that keep to these rules, and one draw needn't show every extreme that they name: `batch_sizes`: every feature has some owner, and every owner some feature, with exactly 128. `bag_ends`: nondecreasing along the last dimension; bags j >= batch_sizes[f, d] are empty; some bag list reaches 256.
All inputs are finite; a program needn't handle non-finite values. No bound on the sum of `labels` on one device may be relied on, other than what follows from the above.
Results may differ from a plain program's by a relative error of at most 0.0095.
Values may be sent and summed in bfloat16 or wider, within the bound.
A program may use at most 192 MiB of HBM per device.

v0:
```python
import jax
import jax.numpy as jnp
from jax import lax
from jax.sharding import PartitionSpec as P

step_size = 32.0


def as_sent(array):

    def short(part):
        return part.astype(jnp.bfloat16) if part.dtype == jnp.float32 else part

    return jax.tree.map(short, array)


def gathered_total(array, axis):
    return lax.all_gather(array, axis).astype(jnp.float32).sum(0)


def bag_members(limits, slot_total):
    starts = jnp.concatenate(
        [jnp.zeros(limits.shape[:-1] + (1,), jnp.int32), limits[..., :-1]], axis=-1
    )
    positions = jnp.arange(slot_total, dtype=jnp.int32)
    inside = (positions >= starts[..., None]) & (positions < limits[..., None])
    return inside.astype(jnp.bfloat16)


def silu_slope(preacts):
    squash = jax.nn.sigmoid(preacts)
    return squash * (1.0 + preacts * (1.0 - squash))


def spread_table(size_table, batch_rows, bag_span):
    chosen = jnp.arange(batch_rows, dtype=jnp.int32) * size_table[..., None] // batch_rows
    return (chosen[..., None] == jnp.arange(bag_span, dtype=jnp.int32)).astype(jnp.bfloat16)


def take_rows(table_one, row_list):
    return table_one[row_list]


def lower_pairs(gram_matrix, vec_count):
    pieces = [gram_matrix[:, index, :index] for index in range(1, vec_count)]
    return jnp.concatenate(pieces, axis=1)


def lower_square(pair_grad, vec_count):
    rows_list = []
    offset = 0
    for index in range(vec_count):
        piece = pair_grad[:, offset : offset + index]
        offset = offset + index
        rows_list.append(jnp.pad(piece, ((0, 0), (0, vec_count - index))))
    return jnp.stack(rows_list, axis=1)


def table_grads(row_list, members, gradient_list, row_total):
    slot_vectors = jnp.einsum(
        "fdks,fdke->fdse", members, gradient_list, preferred_element_type=jnp.float32
    )
    embed_width = gradient_list.shape[-1]

    def one_table(values, row_index):
        return jax.ops.segment_sum(
            values.reshape(-1, embed_width), row_index.reshape(-1), row_total
        )

    return jax.vmap(one_table)(slot_vectors, row_list)


def shards(
    dense,
    small_ids,
    labels,
    small_tables,
    large_tables,
    batch_sizes,
    bag_ends,
    owner_row_index,
    w_first,
    b_first,
    w_out,
):
    groups = lax.axis_size("shard")
    replica = lax.axis_index("rep")
    member_id = lax.axis_index("shard")
    batch_rows, embed_width = dense.shape
    owned_tables, embedding_rows = (large_tables.shape[0], large_tables.shape[1])
    small_count, small_rows = (small_tables.shape[0], small_tables.shape[1])
    feat_count = batch_sizes.shape[0]
    bag_span = bag_ends.shape[2]
    slot_total = owner_row_index.shape[2]
    pair_count = w_first.shape[0] - embed_width
    vec_count = 1 + small_count + feat_count
    first_dest = replica * groups
    own_limits = lax.dynamic_slice_in_dim(bag_ends, first_dest, groups, 1)
    own_rows = lax.dynamic_slice_in_dim(owner_row_index, first_dest, groups, 1)
    recv_sizes = lax.dynamic_slice_in_dim(batch_sizes, first_dest + member_id, 1, 1)[:, 0]
    members = bag_members(own_limits, slot_total)
    collected_rows = jax.vmap(take_rows)(large_tables, own_rows)
    pooled = jnp.einsum(
        "fdks,fdse->fdke", members, collected_rows, preferred_element_type=jnp.float32
    ).astype(jnp.bfloat16)
    arrived = lax.all_to_all(pooled, "shard", split_axis=1, concat_axis=0, tiled=True)
    recv_spread = spread_table(recv_sizes, batch_rows, bag_span)
    large_feat = jnp.einsum(
        "fbj,fje->bfe", recv_spread, arrived[:, 0], preferred_element_type=jnp.float32
    ).astype(jnp.bfloat16)
    small_hot = (small_ids[:, :, None] == jnp.arange(small_rows, dtype=jnp.int32)).astype(
        jnp.bfloat16
    )
    minor_feature = jnp.einsum(
        "btr,tre->bte", small_hot, small_tables, preferred_element_type=jnp.float32
    ).astype(jnp.bfloat16)
    vectors = jnp.concatenate([dense[:, None, :], minor_feature, large_feat], axis=1)
    gram_matrix = jnp.einsum("bie,bje->bij", vectors, vectors, preferred_element_type=jnp.float32)
    pair_values = (lower_pairs(gram_matrix, vec_count) * embed_width ** (-0.5)).astype(jnp.bfloat16)
    features = jnp.concatenate([pair_values, dense], axis=1)
    preact = jnp.dot(features, w_first, preferred_element_type=jnp.float32) + b_first
    hidden = jax.nn.silu(preact)
    logits = jnp.sum(hidden * w_out[None, :], axis=1)
    logit_grad = jax.nn.sigmoid(logits) - labels.astype(jnp.float32)
    pre_grad = (logit_grad[:, None] * w_out[None, :] * silu_slope(preact)).astype(jnp.bfloat16)
    pair_grad = jnp.einsum(
        "bh,ph->bp", pre_grad, w_first[:pair_count], preferred_element_type=jnp.float32
    ) * embed_width ** (-0.5)
    lower_part = lower_square(pair_grad, vec_count)
    symmetric = lower_part + jnp.swapaxes(lower_part, 1, 2)
    vec_grad = jnp.einsum("bij,bje->bie", symmetric, vectors.astype(jnp.float32)).astype(
        jnp.bfloat16
    )
    small_local = jnp.einsum(
        "btr,bte->tre",
        small_hot,
        vec_grad[:, 1 : 1 + small_count],
        preferred_element_type=jnp.float32,
    )
    small_sum = lax.psum(small_local, ("rep", "shard"))
    small_new = (small_tables.astype(jnp.float32) - step_size * small_sum).astype(jnp.bfloat16)
    large_grad_part = vec_grad[:, 1 + small_count :]
    folded = jnp.einsum(
        "fbj,bfe->fje", recv_spread, large_grad_part, preferred_element_type=jnp.float32
    ).astype(jnp.bfloat16)
    accumulate_gradient = lax.all_to_all(
        folded[:, None], "shard", split_axis=0, concat_axis=1, tiled=True
    )
    local_grad = table_grads(own_rows, members, accumulate_gradient, embedding_rows)
    large_grad = jax.tree.map(
        lambda part: part.astype(jnp.float32),
        jax.tree.map(lambda part: gathered_total(part, "rep"), as_sent(local_grad)),
    )
    large_new = (large_tables.astype(jnp.float32) - step_size * large_grad).astype(jnp.bfloat16)
    return (small_new, large_new)


def solution(mesh):
    placed = (
        P(("rep", "shard"), None),
        P(("rep", "shard"), None),
        P(("rep", "shard")),
        P(),
        P("shard", None, None),
        P(),
        P("shard", None, None),
        P("shard", None, None),
        P(),
        P(),
        P(),
    )
    return jax.shard_map(
        shards, mesh=mesh, in_specs=placed, out_specs=(P(), P("shard", None, None)), check_vma=False
    )
```

profile of v0, /device:TPU:1, one launch (start us, length us, event | category | flops | bytes accessed | tf_op | source)
XLA Modules:
  0.0 922.3 jit_solution(10983050159655116990)
XLA Ops:
  11.2 266.0 %gather_fusion = bf16[16384,128]{1,0:T(8,128)(2,1)} fusion(bf16[1,8192,128]{2,1,0:T(8,128)(2,1)} %param.15, s32[16384]{0:T(1024)S(1)} %bitcast.526), kind=kCustom, calls=%fused_computation | custom fusion | bytes 8519680 | tf_op jit(solution)/shard_map/vmap()/gather | solution.py:41
  277.2 6.3 convert_bitcast_fusion.2
  283.5 11.1 %all-to-all-start = ((bf16[1,64,128,128]{3,2,0,1:T(8,128)(2,1)}), bf16[1,64,128,128]{3,2,0,1:T(8,128)(2,1)S(1)}, u32[]{:S(2)}, u32[]{:S(2)}) async-start(bf16[1,64,128,128]{3,2,0,1:T(8,128)(2,1)} %convert_bitcast_fusion.2), calls=%async_computation | async-start | bytes 4194304 | tf_op jit(solution)/shard_map/all_to_all | solution.py:106
  294.9 8.1 convert_bitcast_fusion.3
  303.0 4.1 copy.345
  308.2 15.7 %all-to-all-done = bf16[1,64,128,128]{3,2,0,1:T(8,128)(2,1)S(1)} async-done(((bf16[1,64,128,128]{3,2,0,1:T(8,128)(2,1)}), bf16[1,64,128,128]{3,2,0,1:T(8,128)(2,1)S(1)}, u32[]{:S(2)}, u32[]{:S(2)}) %all-to-all-start) | async-done | bytes 2097184 | tf_op jit(solution)/shard_map/all_to_all | solution.py:106
  323.9 2.1 convert_bitcast_fusion
  326.0 4.8 pad_maximum_fusion
  330.8 10.1 %copy.346 = bf16[256,97,128]{2,1,0:T(8,128)(2,1)} copy(bf16[256,97,128]{0,2,1:T(8,128)(2,1)} %pad_maximum_fusion) | data formatting | bytes 12713984 | tf_op jit(solution)/shard_map/concatenate | solution.py:117
  340.9 13.5 %fusion.60 = f32[256,97,97]{2,1,0:T(8,128)} fusion(bf16[256,97,128]{2,1,0:T(8,128)(2,1)} %copy.346), kind=kOutput, calls=%fused_computation.184 | convolution fusion | flops 616628224 | bytes 15991808 | tf_op jit(solution)/shard_map/bie,bje->bij/dot_general | solution.py:118
  389.2 2.0 slice.808
  391.2 2.0 slice.809
  395.2 2.0 slice.811
  407.0 2.0 slice.817
  411.0 2.0 slice.819
  414.9 2.0 slice.821
  418.9 2.0 slice.823
  420.8 2.0 slice.824
  430.7 2.0 slice.829
  432.7 2.0 slice.830
  434.7 2.0 slice.831
  436.7 2.0 slice.832
  438.7 2.0 slice.833
  440.6 2.0 slice.834
  446.6 2.0 slice.837
  450.5 2.0 slice.839
  452.5 2.0 slice.840
  458.5 2.0 slice.843
  470.3 2.6 slice.849
  472.9 2.0 slice.850
  474.9 2.0 slice.851
  478.8 2.0 slice.853
  482.8 2.0 slice.855
  484.8 2.0 slice.856
  486.8 2.0 slice.857
  494.7 2.0 slice.861
  496.7 2.0 slice.862
  498.7 2.0 slice.863
  502.6 2.0 slice.865
  504.6 2.0 slice.866
  510.5 2.0 slice.869
  514.5 2.0 slice.871
  516.5 2.0 slice.872
  520.5 2.0 slice.874
  526.4 2.0 slice.877
  528.4 14.2 %concatenate.14 = f32[256,4656]{1,0:T(8,128)} concatenate(f32[256,1]{1,0:T(8,128)S(1)} %bitcast.539, f32[256,2]{1,0:T(8,128)S(1)} %bitcast.540, f32[256,3]{1,0:T(8,128)S(1)} %bitcast.541, f32[256,4]{1,0:T(8,128)S(1)} %bitcast.542, f32[256,5]{1,0:T(8,128)S(1)} %bitcast.543, f32[256,6]{1,0:T(8,128)S(1)} %bitcast.544, f32[256,7]{1,0:T(8,128)S(1)} %bitcast.545, ...), dimensions={1} | concatenate | bytes 9535488 | tf_op jit(solution)/shard_map/concatenate | solution.py:46
  542.6 2.9 multiply_convert_fusion
  545.6 6.2 multiply_reduce_fusion
  551.8 3.1 fusion.14
  628.2 15.5 %copy.443 = f32[256,97,97]{1,0,2:T(8,128)} copy(f32[256,97,97]{2,0,1:T(8,128)} %constant_dynamic-update-slice_fusion) | data formatting | bytes 19269632 | tf_op jit(solution)/shard_map/stack | solution.py:56
  643.7 12.3 %bitcast_add_fusion = bf16[256,97,97]{2,0,1:T(8,128)(2,1)} fusion(f32[256,97,97]{2,0,1:T(8,128)} %constant_dynamic-update-slice_fusion, f32[256,97,97]{1,0,2:T(8,128)} %copy.443), kind=kLoop, calls=%fused_computation.7 | loop fusion | flops 4817408 | bytes 24087040 | tf_op jit(solution)/shard_map/add | solution.py:130
  656.1 12.3 %fusion.11 = bf16[256,97,128]{2,1,0:T(8,128)(2,1)} fusion(bf16[256,97,128]{2,1,0:T(8,128)(2,1)S(1)} %bitcast.528, bf16[256,97,97]{2,0,1:T(8,128)(2,1)} %bitcast_add_fusion), kind=kOutput, calls=%fused_computation.20 | convolution fusion | flops 616628224 | bytes 17531392 | tf_op jit(solution)/shard_map/bij,bje->bie/dot_general | solution.py:131
  668.4 2.9 slice.981
  671.3 6.3 fusion
  677.7 5.1 slice.982
  682.8 5.9 convert_bitcast_fusion.1
  688.7 4.7 all-to-all-start.1
  694.2 33.1 %all-to-all-done.1 = bf16[64,1,128,128]{3,2,1,0:T(8,128)(2,1)S(1)} async-done(((bf16[64,1,128,128]{3,2,1,0:T(8,128)(2,1)}), bf16[64,1,128,128]{3,2,1,0:T(8,128)(2,1)S(1)}, u32[]{:S(2)}, u32[]{:S(2)}) %all-to-all-start.1) | async-done | bytes 2097184 | tf_op jit(solution)/shard_map/all_to_all | solution.py:146
  727.2 5.0 fusion.17
  732.2 90.0 %scatter_custom_fusion = f32[8192,128]{1,0:T(8,128)} fusion(s32[16384]{0:T(1024)S(1)} %broadcast_select_fusion, f32[16384,128]{1,0:T(8,128)} %bitcast.529, f32[]{:T(128)} %constant.16.clone.1), kind=kCustom, calls=%fused_computation.43 | custom fusion | flops 2097152 | bytes 4194816
  822.3 3.7 convert_element_type.266
  826.0 75.3 %all-reduce.98.cloned.1.call-done = f32[32,512,128]{2,1,0:T(8,128)} async-done(((f32[32,512,128]{2,1,0:T(8,128)}), f32[32,512,128]{2,1,0:T(8,128)}) %all-reduce.98.cloned.1.call-update) | async-done | bytes 8388624 | tf_op jit(solution)/shard_map/psum | solution.py:140
  901.3 8.0 subtract_convert_fusion
  909.3 3.4 convert_reduce_fusion
  (315 shorter events, 183.5 us)
Async XLA Ops:
  8.0 299.2 %copy-start = (s32[64,128]{1,0:T(8,128)S(1)}, s32[64,128]{1,0:T(8,128)}, u32[]{:S(2)}) copy-start(s32[64,128]{1,0:T(8,128)} %param.16) | copy-start | bytes 98308
  9.6 267.6 %copy-start.4 = (s32[64,128]{1,0:T(8,128)}, s32[64,128]{1,0:T(8,128)S(1)}, u32[]{:S(2)}) copy-start(s32[64,128]{1,0:T(8,128)S(1)} %get-tuple-element.7) | copy-start | bytes 98308
  277.2 17.7 %copy-start.11 = (s32[256,32]{0,1:T(8,128)S(1)}, s32[256,32]{0,1:T(8,128)}, u32[]{:S(2)}) copy-start(s32[256,32]{0,1:T(8,128)} %param.12) | copy-start | bytes 98308
  283.5 23.6 %copy-start.6 = (bf16[256,128]{1,0:T(8,128)(2,1)S(1)}, bf16[256,128]{1,0:T(8,128)(2,1)}, u32[]{:S(2)}) copy-start(bf16[256,128]{1,0:T(8,128)(2,1)} %param.11) | copy-start | bytes 196612
  283.5 40.4 %all-to-all-start = ((bf16[1,64,128,128]{3,2,0,1:T(8,128)(2,1)}), bf16[1,64,128,128]{3,2,0,1:T(8,128)(2,1)S(1)}, u32[]{:S(2)}, u32[]{:S(2)}) async-start(bf16[1,64,128,128]{3,2,0,1:T(8,128)(2,1)} %convert_bitcast_fusion.2), calls=%async_computation | async-start | bytes 4194304 | tf_op jit(solution)/shard_map/all_to_all | solution.py:106
  294.5 606.7 %all-reduce.98.cloned.1.call-start = ((), (), s32[]{:S(2)}) async-start(), calls=%async_computation.2 | async-start | bytes 16777216 | tf_op jit(solution)/shard_map/psum | solution.py:140
  524.4 21.1 %copy-start.13 = (f32[1024]{0:T(1024)S(1)}, f32[1024]{0:T(1024)}, u32[]{:S(2)}) copy-start(f32[1024]{0:T(1024)} %param.20) | copy-start | bytes 12292
  524.4 21.1 %copy-start.14 = (f32[1024]{0:T(1024)S(1)}, f32[1024]{0:T(1024)}, u32[]{:S(2)}) copy-start(f32[1024]{0:T(1024)} %param.21) | copy-start | bytes 12292
  542.6 9.2 slice-start.2
  545.5 6.2 copy-start.7
  545.5 6.3 slice-start.3
  545.6 6.3 slice-start.4
  554.9 9.9 %copy-start.10 = (pred[97]{0:T(512)(128)(4,1)S(1)}, pred[97]{0:T(512)(128)(4,1)}, u32[]{:S(2)}) copy-start(pred[97]{0:T(512)(128)(4,1)} %constant.17.clone.1) | copy-start | bytes 295
  628.2 27.8 %slice-start = ((s8[6815744]{0:T(1024)(128)(4,1)}), s8[2621440]{0:T(1024)(128)(4,1)S(1)}, s32[]{:S(2)}) async-start(s8[6815744]{0:T(1024)(128)(4,1)} %bitcast.527), calls=%async_computation.4 | async-start | bytes 5242880
  643.7 12.3 %slice-start.1 = ((s8[6815744]{0:T(1024)(128)(4,1)}), s8[4194304]{0:T(1024)(128)(4,1)S(1)}, s32[]{:S(2)}) async-start(s8[6815744]{0:T(1024)(128)(4,1)} %bitcast.527), calls=%async_computation.5 | async-start | bytes 8388608
  656.1 15.2 %copy-start.12 = (s32[256,32]{0,1:T(8,128)S(1)}, s32[256,32]{0,1:T(8,128)}, u32[]{:S(2)}) copy-start(s32[256,32]{0,1:T(8,128)} %param.12) | copy-start | bytes 98308
  677.6 15.8 %copy-start.3 = (s32[1,64,256]{2,1,0:T(8,128)S(1)}, s32[1,64,256]{2,1,0:T(8,128)}, u32[]{:S(2)}) copy-start(s32[1,64,256]{2,1,0:T(8,128)} %get-tuple-element.3) | copy-start | bytes 196612
  677.6 15.9 %copy-start.9 = (s32[2]{0:T(128)S(1)}, s32[2]{0:T(128)}, u32[]{:S(2)}) copy-start(s32[2]{0:T(128)} %constant.246) | copy-start | bytes 28
  677.6 16.2 %copy-start.8 = (s32[2]{0:T(128)S(1)}, s32[2]{0:T(128)}, u32[]{:S(2)}) copy-start(s32[2]{0:T(128)} %constant.249) | copy-start | bytes 28
  677.7 49.6 %copy-start.5 = (s32[64,128]{1,0:T(8,128)S(1)}, s32[64,128]{1,0:T(8,128)}, u32[]{:S(2)}) copy-start(s32[64,128]{1,0:T(8,128)} %copy-done.4) | copy-start | bytes 98308
  688.7 38.5 %all-to-all-start.1 = ((bf16[64,1,128,128]{3,2,1,0:T(8,128)(2,1)}), bf16[64,1,128,128]{3,2,1,0:T(8,128)(2,1)S(1)}, u32[]{:S(2)}, u32[]{:S(2)}) async-start(bf16[64,1,128,128]{3,2,1,0:T(8,128)(2,1)} %convert_bitcast_fusion.1), calls=%async_computation.1 | async-start | bytes 4194304 | tf_op jit(solution)/shard_map/all_to_all | solution.py:146
  693.4 215.9 %all-gather.3.cloned.1.call-start = ((), (), s32[]{:S(2)}) async-start(), calls=%async_computation.3 | async-start | bytes 6291456 | tf_op jit(solution)/shard_map/all_gather | solution.py:18
  826.0 86.7 %copy-start.2 = (bf16[1,8192,128]{2,1,0:T(8,128)(2,1)S(1)}, bf16[1,8192,128]{2,1,0:T(8,128)(2,1)}, u32[]{:S(2)}) copy-start(bf16[1,8192,128]{2,1,0:T(8,128)(2,1)} %param.15) | copy-start | bytes 6291460
  826.0 88.7 %copy-start.1 = (s32[64,128]{1,0:T(8,128)S(1)}, s32[64,128]{1,0:T(8,128)}, u32[]{:S(2)}) copy-start(s32[64,128]{1,0:T(8,128)} %param.16) | copy-start | bytes 98308
Sparse Core Ops, SparseCore 0:
  677.7 223.4 all-reduce.97
Sparse Core Ops, SparseCore 1:
  826.1 61.7 all-gather.2
where the time goes:
time: 933 us; the launch traced here: 922 us
  local copies, waits for them, and re-layouts  566 us (61%)
  other arithmetic  130 us (14%)
  waiting for transfers between devices  124 us (13%)
  matrix products  68.6 us (7%)
  between operations  17 us (2%)
  starting transfers between devices  16.1 us (2%)
    gather x2, local copies, waits for them, and re-layouts, take_rows(): return table_one[row_list]  266 us
    slice x96, local copies, waits for them, and re-layouts, lower_pairs(): pieces = [gram_matrix[:, index, :index] for index in range(1, vec_count)]  174 us
    unnamed x8, other arithmetic  91.3 us
    psum x1, waiting for transfers between devices, shards(): small_sum = lax.psum(small_local, ('rep', 'shard'))  75.3 us
    unnamed x137, local copies, waits for them, and re-layouts  63 us
    all_to_all x1, waiting for transfers between devices, shards(): lax.all_to_all(folded[:, None], 'shard', split_axis=0, concat_axis=1, til...  33.1 us
  transfers between devices with their start and end apart: 4, of which 3 were waited for; matrix products, arithmetic and copies ran while one was open for 14% of the time, Pallas kernels for 0%

commit v1 on v0

--- a/solution.py
+++ b/solution.py
@@ -137,7 +137,7 @@
         vec_grad[:, 1 : 1 + small_count],
         preferred_element_type=jnp.float32,
     )
-    small_sum = lax.psum(small_local, ("rep", "shard"))
+    small_sum = lax.psum(lax.psum(small_local, "rep"), "shard")
     small_new = (small_tables.astype(jnp.float32) - step_size * small_sum).astype(jnp.bfloat16)
     large_grad_part = vec_grad[:, 1 + small_count :]
     folded = jnp.einsum(

time: 933 us -> 1570 us (1.68)
  waiting for transfers between devices: 124 us -> 761 us
    psum x1 -> x2, waiting for transfers between devices: 75.3 us -> 654 us  [shards(): small_sum = lax.psum(lax.psum(small_local, 'rep'), 'shard')]
    all_gather x1, waiting for transfers between devices: 0.01 us -> 62.7 us  [gathered_total(): return lax.all_gather(array, axis).astype(jnp.float32).sum(0)]
  transfers between devices with their start and end apart: 4 -> 5, of which waited for: 3 -> 5; matrix products, arithmetic and copies ran while one was open for 14% -> 8% of each run, Pallas kernels for 0% -> 0%
where the time goes in v1:
time: 1570 us; the launch traced here: 1560 us
  waiting for transfers between devices  761 us (48%)
  local copies, waits for them, and re-layouts  566 us (36%)
  other arithmetic  130 us (8%)
  matrix products  68.6 us (4%)
  starting transfers between devices  16.2 us (1%)
    psum x2, waiting for transfers between devices, shards(): small_sum = lax.psum(lax.psum(small_local, 'rep'), 'shard')  654 us
    gather x2, local copies, waits for them, and re-layouts, take_rows(): return table_one[row_list]  266 us
    slice x96, local copies, waits for them, and re-layouts, lower_pairs(): pieces = [gram_matrix[:, index, :index] for index in range(1, vec_count)]  174 us
    unnamed x8, other arithmetic  91.3 us
    unnamed x137, local copies, waits for them, and re-layouts  63 us
    all_gather x1, waiting for transfers between devices, gathered_total(): return lax.all_gather(array, axis).astype(jnp.float32).sum(0)  62.7 us
  transfers between devices with their start and end apart: 5, of which 5 were waited for; matrix products, arithmetic and copies ran while one was open for 8% of the time, Pallas kernels for 0%

profile of v1, /device:TPU:1, one launch (start us, length us, event | category | flops | bytes accessed | tf_op | source)
XLA Modules:
  0.0 1557.7 jit_solution(10474751178959603138)
XLA Ops:
  10.4 266.0 %gather_fusion = bf16[16384,128]{1,0:T(8,128)(2,1)} fusion(bf16[1,8192,128]{2,1,0:T(8,128)(2,1)} %param.15, s32[16384]{0:T(1024)S(1)} %bitcast.526), kind=kCustom, calls=%fused_computation | custom fusion | bytes 8519680 | tf_op jit(solution)/shard_map/vmap()/gather | solution.py:41
  276.4 6.3 convert_bitcast_fusion.2
  282.6 11.1 all-to-all-start
  294.1 8.1 convert_bitcast_fusion.3
  302.1 4.1 copy.345
  307.4 15.7 %all-to-all-done = bf16[1,64,128,128]{3,2,0,1:T(8,128)(2,1)S(1)} async-done(((bf16[1,64,128,128]{3,2,0,1:T(8,128)(2,1)}), bf16[1,64,128,128]{3,2,0,1:T(8,128)(2,1)S(1)}, u32[]{:S(2)}, u32[]{:S(2)}) %all-to-all-start) | async-done | bytes 2097184 | tf_op jit(solution)/shard_map/all_to_all | solution.py:106
  323.0 2.1 convert_bitcast_fusion
  325.2 4.8 pad_maximum_fusion
  330.0 10.1 copy.346
  340.1 13.5 fusion.60
  388.4 2.0 slice.808
  390.4 2.0 slice.809
  394.3 2.0 slice.811
  406.2 2.0 slice.817
  414.0 2.0 slice.821
  418.0 2.0 slice.823
  420.0 2.0 slice.824
  429.9 2.0 slice.829
  431.9 2.0 slice.830
  433.9 2.0 slice.831
  435.8 2.0 slice.832
  437.8 2.0 slice.833
  439.8 2.0 slice.834
  445.7 2.0 slice.837
  449.7 2.0 slice.839
  451.7 2.0 slice.840
  457.6 2.0 slice.843
  469.5 2.6 slice.849
  472.1 2.0 slice.850
  474.1 2.0 slice.851
  478.0 2.0 slice.853
  482.0 2.0 slice.855
  484.0 2.0 slice.856
  485.9 2.0 slice.857
  493.8 2.0 slice.861
  495.8 2.0 slice.862
  497.8 2.0 slice.863
  501.8 2.0 slice.865
  503.8 2.0 slice.866
  509.7 2.0 slice.869
  515.7 2.0 slice.872
  519.6 2.0 slice.874
  525.5 2.0 slice.877
  527.5 14.2 concatenate.14
  541.8 2.9 multiply_convert_fusion
  544.7 6.2 multiply_reduce_fusion
  551.0 3.1 fusion.14
  627.4 15.5 copy.443
  642.9 12.3 bitcast_add_fusion
  655.3 12.3 fusion.11
  667.5 2.9 slice.981
  670.5 6.3 fusion
  676.8 5.1 slice.982
  682.0 5.9 convert_bitcast_fusion.1
  687.9 4.7 all-to-all-start.1
  693.3 28.6 %all-to-all-done.1 = bf16[64,1,128,128]{3,2,1,0:T(8,128)(2,1)S(1)} async-done(((bf16[64,1,128,128]{3,2,1,0:T(8,128)(2,1)}), bf16[64,1,128,128]{3,2,1,0:T(8,128)(2,1)S(1)}, u32[]{:S(2)}, u32[]{:S(2)}) %all-to-all-start.1) | async-done | bytes 2097184 | tf_op jit(solution)/shard_map/all_to_all | solution.py:146
  721.9 5.0 fusion.17
  726.9 90.0 %scatter_custom_fusion = f32[8192,128]{1,0:T(8,128)} fusion(s32[16384]{0:T(1024)S(1)} %broadcast_select_fusion, f32[16384,128]{1,0:T(8,128)} %bitcast.529, f32[]{:T(128)} %constant.16.clone.1), kind=kCustom, calls=%fused_computation.43 | custom fusion | flops 2097152 | bytes 4194816
  816.9 3.9 convert_element_type.266
  820.9 83.2 %all-reduce.99.cloned.1.call-done = f32[32,512,128]{2,1,0:T(8,128)} async-done(((f32[32,512,128]{2,1,0:T(8,128)}), f32[32,512,128]{2,1,0:T(8,128)}) %all-reduce.99.cloned.1.call-update) | async-done | bytes 8388624 | tf_op jit(solution)/shard_map/psum | solution.py:140
  904.1 62.7 %all-gather.3.cloned.1.call-done = bf16[16384,128]{1,0:T(8,128)(2,1)} async-done(((bf16[8192,128]{1,0:T(8,128)(2,1)}), bf16[16384,128]{1,0:T(8,128)(2,1)}) %all-gather.3.cloned.1.call-update) | async-done | bytes 4194320 | tf_op jit(solution)/shard_map/all_gather | solution.py:18
  966.8 3.4 convert_reduce_fusion
  972.1 570.8 %all-reduce.101.cloned.1.call-done = f32[32,512,128]{2,1,0:T(8,128)} async-done(((f32[32,512,128]{2,1,0:T(8,128)}), f32[32,512,128]{2,1,0:T(8,128)}) %all-reduce.101.cloned.1.call-update) | async-done | bytes 8388624 | tf_op jit(solution)/shard_map/psum | solution.py:140
  1543.0 8.0 subtract_convert_fusion
  (318 shorter events, 187.5 us)
Async XLA Ops:
  7.2 299.2 %copy-start = (s32[64,128]{1,0:T(8,128)S(1)}, s32[64,128]{1,0:T(8,128)}, u32[]{:S(2)}) copy-start(s32[64,128]{1,0:T(8,128)} %param.16) | copy-start | bytes 98308
  8.8 267.6 %copy-start.4 = (s32[64,128]{1,0:T(8,128)}, s32[64,128]{1,0:T(8,128)S(1)}, u32[]{:S(2)}) copy-start(s32[64,128]{1,0:T(8,128)S(1)} %get-tuple-element.7) | copy-start | bytes 98308
  276.4 17.7 %copy-start.11 = (s32[256,32]{0,1:T(8,128)S(1)}, s32[256,32]{0,1:T(8,128)}, u32[]{:S(2)}) copy-start(s32[256,32]{0,1:T(8,128)} %param.12) | copy-start | bytes 98308
  282.6 23.6 %copy-start.6 = (bf16[256,128]{1,0:T(8,128)(2,1)S(1)}, bf16[256,128]{1,0:T(8,128)(2,1)}, u32[]{:S(2)}) copy-start(bf16[256,128]{1,0:T(8,128)(2,1)} %param.11) | copy-start | bytes 196612
  282.6 40.4 %all-to-all-start = ((bf16[1,64,128,128]{3,2,0,1:T(8,128)(2,1)}), bf16[1,64,128,128]{3,2,0,1:T(8,128)(2,1)S(1)}, u32[]{:S(2)}, u32[]{:S(2)}) async-start(bf16[1,64,128,128]{3,2,0,1:T(8,128)(2,1)} %convert_bitcast_fusion.2), calls=%async_computation | async-start | bytes 4194304 | tf_op jit(solution)/shard_map/all_to_all | solution.py:106
  293.7 610.3 %all-reduce.99.cloned.1.call-start = ((), (), s32[]{:S(2)}) async-start(), calls=%async_computation.2 | async-start | bytes 16777216 | tf_op jit(solution)/shard_map/psum | solution.py:140
  523.6 21.1 %copy-start.13 = (f32[1024]{0:T(1024)S(1)}, f32[1024]{0:T(1024)}, u32[]{:S(2)}) copy-start(f32[1024]{0:T(1024)} %param.20) | copy-start | bytes 12292
  523.6 21.1 %copy-start.14 = (f32[1024]{0:T(1024)S(1)}, f32[1024]{0:T(1024)}, u32[]{:S(2)}) copy-start(f32[1024]{0:T(1024)} %param.21) | copy-start | bytes 12292
  541.7 9.2 slice-start.2
  544.7 6.2 copy-start.7
  544.7 6.3 slice-start.3
  544.7 6.3 slice-start.4
  554.1 9.9 copy-start.10
  627.4 27.8 %slice-start = ((s8[6815744]{0:T(1024)(128)(4,1)}), s8[2621440]{0:T(1024)(128)(4,1)S(1)}, s32[]{:S(2)}) async-start(s8[6815744]{0:T(1024)(128)(4,1)} %bitcast.527), calls=%async_computation.5 | async-start | bytes 5242880
  642.9 12.3 slice-start.1
  655.3 15.2 copy-start.12
  676.8 15.8 %copy-start.3 = (s32[1,64,256]{2,1,0:T(8,128)S(1)}, s32[1,64,256]{2,1,0:T(8,128)}, u32[]{:S(2)}) copy-start(s32[1,64,256]{2,1,0:T(8,128)} %get-tuple-element.3) | copy-start | bytes 196612
  676.8 15.9 %copy-start.9 = (s32[2]{0:T(128)S(1)}, s32[2]{0:T(128)}, u32[]{:S(2)}) copy-start(s32[2]{0:T(128)} %constant.246) | copy-start | bytes 28
  676.8 16.2 %copy-start.8 = (s32[2]{0:T(128)S(1)}, s32[2]{0:T(128)}, u32[]{:S(2)}) copy-start(s32[2]{0:T(128)} %constant.249) | copy-start | bytes 28
  676.8 45.1 %copy-start.5 = (s32[64,128]{1,0:T(8,128)S(1)}, s32[64,128]{1,0:T(8,128)}, u32[]{:S(2)}) copy-start(s32[64,128]{1,0:T(8,128)} %copy-done.4) | copy-start | bytes 98308
  687.9 34.0 %all-to-all-start.1 = ((bf16[64,1,128,128]{3,2,1,0:T(8,128)(2,1)}), bf16[64,1,128,128]{3,2,1,0:T(8,128)(2,1)S(1)}, u32[]{:S(2)}, u32[]{:S(2)}) async-start(bf16[64,1,128,128]{3,2,1,0:T(8,128)(2,1)} %convert_bitcast_fusion.1), calls=%async_computation.1 | async-start | bytes 4194304 | tf_op jit(solution)/shard_map/all_to_all | solution.py:146
  692.6 274.2 %all-gather.3.cloned.1.call-start = ((), (), s32[]{:S(2)}) async-start(), calls=%async_computation.4 | async-start | bytes 6291456 | tf_op jit(solution)/shard_map/all_gather | solution.py:18
  816.9 153.2 %copy-start.2 = (bf16[1,8192,128]{2,1,0:T(8,128)(2,1)S(1)}, bf16[1,8192,128]{2,1,0:T(8,128)(2,1)}, u32[]{:S(2)}) copy-start(bf16[1,8192,128]{2,1,0:T(8,128)(2,1)} %param.15) | copy-start | bytes 6291460
  820.8 722.2 %all-reduce.101.cloned.1.call-start = ((), (), s32[]{:S(2)}) async-start(), calls=%async_computation.3 | async-start | bytes 16777216 | tf_op jit(solution)/shard_map/psum | solution.py:140
  966.8 584.2 %copy-start.1 = (s32[64,128]{1,0:T(8,128)S(1)}, s32[64,128]{1,0:T(8,128)}, u32[]{:S(2)}) copy-start(s32[64,128]{1,0:T(8,128)} %param.16) | copy-start | bytes 98308
Sparse Core Ops, SparseCore 0:
  676.9 227.0 all-reduce.98
  906.3 60.4 all-gather.2
  969.3 573.6 all-reduce.100
